TPU v7x, 512 devices: a whole 4x8x8 slice. The times are simulated.
512 devices in a mesh: dp: 64 (over z, y), tensor: 8 (over x, core).
Axes of the slice: x: 4, y: 8, z: 8, core: 2. Of those that a mesh axis runs over, the one named last changes fastest.
Arguments:
- gradient: bfloat16 [64, 512, 8192], P('dp', 'tensor'), may hold values from -110 to 110
- momentum: bfloat16 [64, 512, 8192], P('dp', 'tensor'), may hold values from -6 to 6
- indices: int32 [64, 8, 128, 32], P('dp', 'tensor'), may hold values from 0 to 4095, all different within a row
Outputs:
- new_momentum: bfloat16 [64, 512, 8192], P('dp', 'tensor')
- update: bfloat16 [512, 8192], P('tensor')
Inputs may be any that keep to these rules, and one draw needn't show every extreme that they name: The 32 indices of one span of one replica are distinct; index a * 64 + b names row frequency a and column frequency b.
All inputs are finite; a program needn't handle non-finite values.
Results may differ from a plain program's by a relative error of at most 0.0049.
Values may be sent and summed in bfloat16 or wider, within the bound.
A program may use at most 64 MiB of HBM per device.

v0:
```python
import jax
import jax.numpy as jnp
from jax import lax
from jax.sharding import Mesh
from jax.sharding import PartitionSpec as P

BLOCK = 64
TENSOR = ("tensor_0", "tensor_1")
DP = ("dp_0", "dp_1")
DP_TENSOR = ("dp_0", "dp_1", "tensor_0", "tensor_1")


EPSILON = 1e-06
DECAY = 0.999


def one_axis_at_a_time(value, axes):
    for axis in axes:
        value = lax.psum(value, axis)
    return value


def laid_out(pieces, dim):
    pieces = jnp.moveaxis(pieces, 0, dim)
    shape = pieces.shape
    return pieces.reshape(*shape[:dim], shape[dim] * shape[dim + 1], *shape[dim + 2 :])


def from_everyone(value, axis):
    copies = jnp.broadcast_to(value, (lax.axis_size(axis), *value.shape))
    return lax.all_to_all(copies, axis, split_axis=0, concat_axis=0, tiled=True)


def gather_directly(value, axis, dim):
    return laid_out(from_everyone(value, axis), dim)


def dct_basis(block_edge):
    frequency = jnp.arange(block_edge, dtype=jnp.float32)[:, None]
    position = jnp.arange(block_edge, dtype=jnp.float32)[None, :]
    waves = jnp.cos(jnp.pi * (2.0 * position + 1.0) * frequency / (2.0 * block_edge))
    weights = jnp.where(frequency == 0.0, jnp.sqrt(1.0 / block_edge), jnp.sqrt(2.0 / block_edge))
    return waves * weights


def to_spans(slab, block_edge):
    height, columns = slab.shape
    shaped = slab.reshape(height // block_edge, block_edge, columns // block_edge, block_edge)
    return shaped.transpose(0, 2, 1, 3).reshape(-1, block_edge, block_edge)


def from_spans(blocks, height, columns):
    block_edge = blocks.shape[-1]
    shaped = blocks.reshape(height // block_edge, columns // block_edge, block_edge, block_edge)
    return shaped.transpose(0, 2, 1, 3).reshape(height, columns)


def inverse(spectra, cosines):
    return jnp.einsum("ka,ckl,lb->cab", cosines, spectra, cosines, precision=lax.Precision.HIGHEST)


def densify(shipped, chosen, block_edge):
    sources, number, selected = shipped.shape
    merged_values = shipped.transpose(1, 0, 2).reshape(number, sources * selected)
    merged_ids = chosen.transpose(1, 0, 2).reshape(number, sources * selected)
    levels = jnp.arange(block_edge, dtype=jnp.int32)[None, :, None]
    row_hits = jnp.where(
        (merged_ids // block_edge)[:, None, :] == levels,
        merged_values[:, None, :],
        jnp.zeros((), jnp.bfloat16),
    )
    col_hits = ((merged_ids % block_edge)[:, None, :] == levels).astype(jnp.bfloat16)
    return jnp.einsum("caj,cbj->cab", row_hits, col_hits, preferred_element_type=jnp.float32)


def local(gradient, momentum, indices):
    block_edge = BLOCK
    cosines = dct_basis(block_edge)
    precise = lax.Precision.HIGHEST
    height = gradient.shape[1]
    columns = gradient.shape[2]
    renewed = DECAY * momentum[0].astype(jnp.float32) + gradient[0].astype(jnp.float32)
    spectra = jnp.einsum(
        "ka,cab,lb->ckl", cosines, to_spans(renewed, block_edge), cosines, precision=precise
    )
    span_count = spectra.shape[0]
    chosen = indices[0].reshape(span_count, indices.shape[-1])
    levels = jnp.arange(block_edge, dtype=jnp.int32)[None, None, :]
    row_pick = ((chosen // block_edge)[:, :, None] == levels).astype(jnp.float32)
    col_pick = ((chosen % block_edge)[:, :, None] == levels).astype(jnp.float32)
    partial_value = jnp.einsum("cka,cab->ckb", row_pick, spectra, precision=precise)
    picked = jnp.sum(partial_value * col_pick, axis=2)
    marker = jnp.einsum("cka,ckb->cab", row_pick, col_pick, precision=precise)
    restored = inverse(spectra * marker, cosines)
    new_momentum = (renewed - from_spans(restored, height, columns)).astype(jnp.bfloat16)[None]
    values = picked.astype(jnp.bfloat16)
    element_total = height * columns * lax.axis_size(TENSOR)
    replicas = lax.axis_size(DP)
    owned_count = span_count // replicas
    outgoing = (
        values.reshape(replicas, owned_count, -1),
        chosen.reshape(replicas, owned_count, -1),
    )
    owned = inverse(
        densify(
            lax.all_to_all(outgoing[0], DP, split_axis=0, concat_axis=0, tiled=True),
            lax.all_to_all(outgoing[1], DP, split_axis=0, concat_axis=0, tiled=True),
            block_edge,
        ),
        cosines,
    )
    energy = one_axis_at_a_time(jnp.sum(owned * owned), DP_TENSOR)
    scaled = (owned / jnp.sqrt(energy / element_total + EPSILON)).astype(jnp.bfloat16)
    whole = gather_directly(scaled, DP, 0)
    update = from_spans(whole, height, columns)
    return (new_momentum, update)


def solution(mesh):
    split = Mesh(mesh.devices.reshape(8, 8, 4, 2), ("dp_0", "dp_1", "tensor_0", "tensor_1"))
    placed = (P(DP, TENSOR, None), P(DP, TENSOR, None), P(DP, TENSOR, None, None))
    return jax.shard_map(
        local,
        mesh=split,
        in_specs=placed,
        out_specs=(P(DP, TENSOR, None), P(TENSOR, None)),
        check_vma=False,
    )
```

profile of v0, /device:TPU:8, one launch (start us, length us, event | category | flops | bytes accessed | tf_op | source)
XLA Modules:
  0.0 181.7 jit_solution(11154151874710446193)
XLA Ops:
  0.6 1.8 %convert_add_fusion = f32[1,64,8192]{2,1,0:T(8,128)S(1)} fusion(bf16[1,64,8192]{2,1,0:T(8,128)(2,1)} %param.3, bf16[1,64,8192]{2,1,0:T(8,128)(2,1)} %param.4), kind=kLoop, calls=%fused_computation.12 | loop fusion | flops 2097152 | bytes 4194304 | tf_op jit(solution)/shard_map/add | solution.py:82
  2.5 3.0 %add.77 = f32[1,64,128,64]{3,2,1,0:T(8,128)} reshape(f32[1,64,8192]{2,1,0:T(8,128)S(1)} %convert_add_fusion) | data formatting | bytes 4194304 | tf_op jit(solution)/shard_map/add | solution.py:82
  5.5 0.0 copy-start.1
  5.5 3.5 %copy.36 = f32[128,64,64]{0,1,2:T(8,128)S(1)} copy(f32[128,64,64]{2,0,1:T(8,128)} %bitcast.70) | data formatting | bytes 4194304 | tf_op jit(solution)/shard_map/reshape | solution.py:49
  9.0 0.0 copy-done.1
  9.0 0.1 copy.38
  9.1 0.1 copy.39
  9.2 4.3 %fusion.6 = f32[128,64,64]{2,1,0:T(8,128)} fusion(s32[128,32]{1,0:T(8,128)S(1)} %copy.39, s32[128,32]{1,0:T(8,128)S(1)} %copy.38), kind=kOutput, calls=%fused_computation.9 | convolution fusion | flops 34078720 | bytes 2129920 | tf_op jit(solution)/shard_map/cka,ckb->cab/dot_general | solution.py:93
  13.6 4.8 %copy.40 = f32[128,64,64]{0,2,1:T(8,128)} copy(f32[128,64,64]{2,1,0:T(8,128)} %fusion.6) | data formatting | bytes 4194304 | tf_op jit(solution)/shard_map/cka,ckb->cab/dot_general | solution.py:93
  18.4 0.0 copy-start
  18.4 2.1 %fusion.28 = f32[128,64,64]{0,2,1:T(8,128)S(1)} fusion(f32[128,64,64]{0,1,2:T(8,128)S(1)} %copy.36, f32[64]{0:T(128)S(1)} %get-tuple-element.10, f32[64]{0:T(128)S(1)} %get-tuple-element.11), kind=kOutput, calls=%fused_computation.34 | convolution fusion | flops 402665472 | bytes 4194816 | tf_op jit(solution)/shard_map/ka,cab,lb->ckl/dot_general | solution.py:83
  20.5 0.0 copy-done
  20.5 4.7 %fusion.58 = (f32[128,64,64]{0,2,1:T(8,128)S(1)}, f32[128,64,64]{0,2,1:T(8,128)}) fusion(f32[128,64,64]{0,2,1:T(8,128)S(1)} %copy-done, f32[64]{0:T(128)S(1)} %get-tuple-element.10, f32[64]{0:T(128)S(1)} %get-tuple-element.11, f32[128,64,64]{0,2,1:T(8,128)S(1)} %fusion.28), kind=kOutput, calls=%fused_computation.81 | convolution fusion | flops 403189760 | bytes 8389120 | tf_op jit(solution)/shard_map/ka,cab,lb->ckl/dot_general | solution.py:83
  25.3 5.6 %copy.48 = f32[128,64,64]{2,1,0:T(8,128)} copy(f32[128,64,64]{0,2,1:T(8,128)} %get-tuple-element.7) | data formatting | bytes 4194304 | tf_op jit(solution)/shard_map/ka,cab,lb->ckl/dot_general | solution.py:83
  30.9 5.8 %select_reduce_fusion = bf16[128,32]{1,0:T(8,128)(2,1)} fusion(f32[128,64,64]{2,1,0:T(8,128)} %copy.48, s32[128,32]{1,0:T(8,128)S(1)} %copy.39, s32[128,32]{1,0:T(8,128)S(1)} %copy.38), kind=kOutput, calls=%fused_computation.6 | convolution fusion | flops 202371072 | bytes 2138112 | tf_op jit(solution)/shard_map/cka,cab->ckb/dot_general | solution.py:91
  36.7 16.8 %all-to-all-start.1 = ((bf16[64,2,32]{2,1,0:T(2,128)(2,1)}), bf16[64,2,32]{2,1,0:T(2,128)(2,1)S(1)}, u32[]{:S(2)}, u32[]{:S(2)}) async-start(bf16[64,2,32]{2,1,0:T(2,128)(2,1)} %bitcast.10), calls=%async_computation.1 | async-start | bytes 65536 | tf_op jit(solution)/shard_map/all_to_all | solution.py:106
  53.4 0.7 copy.46
  54.2 10.2 %all-to-all-done.1 = bf16[64,2,32]{2,1,0:T(2,128)(2,1)S(1)} async-done(((bf16[64,2,32]{2,1,0:T(2,128)(2,1)}), bf16[64,2,32]{2,1,0:T(2,128)(2,1)S(1)}, u32[]{:S(2)}, u32[]{:S(2)}) %all-to-all-start.1) | async-done | bytes 8224 | tf_op jit(solution)/shard_map/all_to_all | solution.py:106
  64.4 5.5 %all-to-all-start = ((s32[64,2,32]{2,1,0:T(2,128)}), s32[64,2,32]{2,1,0:T(2,128)S(1)}, u32[]{:S(2)}, u32[]{:S(2)}) async-start(s32[64,2,32]{2,1,0:T(2,128)} %bitcast.8), calls=%async_computation | async-start | bytes 131072 | tf_op jit(solution)/shard_map/all_to_all | solution.py:107
  69.9 0.1 broadcast_in_dim.36
  70.0 11.4 %all-to-all-done = s32[64,2,32]{2,1,0:T(2,128)S(1)} async-done(((s32[64,2,32]{2,1,0:T(2,128)}), s32[64,2,32]{2,1,0:T(2,128)S(1)}, u32[]{:S(2)}, u32[]{:S(2)}) %all-to-all-start) | async-done | bytes 16416 | tf_op jit(solution)/shard_map/all_to_all | solution.py:107
  81.4 0.1 reshape.173
  81.5 0.1 and_select_fusion.1
  81.6 0.3 fusion.15
  81.9 0.5 fusion.25
  82.4 0.9 multiply_reduce_fusion
  83.3 15.4 %psum.28 = f32[]{:T(128)} all-reduce(f32[]{:T(128)} %get-tuple-element.8), channel_id=1, replica_groups=mesh['dp_0'=8,'dp_1'=8,'tensor_0'=4,'tensor_1'=2] {'dp_0'}, use_global_device_ids=true, to_apply=%region_2.3 | all-reduce | flops 1 | bytes 8 | tf_op jit(solution)/shard_map/psum | solution.py:19
  98.7 16.0 %psum.29 = f32[]{:T(128)} all-reduce(f32[]{:T(128)} %psum.28), channel_id=1, replica_groups=mesh['dp_0'=8,'dp_1'=8,'tensor_0'=4,'tensor_1'=2] {'dp_1'}, use_global_device_ids=true, to_apply=%region_3.4 | all-reduce | flops 1 | bytes 8 | tf_op jit(solution)/shard_map/psum | solution.py:19
  114.7 11.1 %psum.30 = f32[]{:T(128)} all-reduce(f32[]{:T(128)} %psum.29), channel_id=1, replica_groups=mesh['dp_0'=8,'dp_1'=8,'tensor_0'=4,'tensor_1'=2] {'tensor_0'}, use_global_device_ids=true, to_apply=%region_4.5 | all-reduce | flops 1 | bytes 8 | tf_op jit(solution)/shard_map/psum | solution.py:19
  125.8 4.8 %fusion.2 = f32[128,64,64]{0,2,1:T(8,128)} fusion(f32[128,64,64]{0,2,1:T(8,128)S(1)} %get-tuple-element.6, f32[64]{0:T(128)S(1)} %get-tuple-element.10, f32[64]{0:T(128)S(1)} %get-tuple-element.11), kind=kOutput, calls=%fused_computation.2 | convolution fusion | flops 402665472 | bytes 4194816 | tf_op jit(solution)/shard_map/ka,ckl,lb->cab/dot_general | solution.py:59
  130.6 3.1 %psum.31 = f32[]{:T(128)} all-reduce(f32[]{:T(128)} %psum.30), channel_id=1, replica_groups=mesh['dp_0'=8,'dp_1'=8,'tensor_0'=4,'tensor_1'=2] {'tensor_1'}, use_global_device_ids=true, to_apply=%region_5.6 | all-reduce | flops 1 | bytes 8 | tf_op jit(solution)/shard_map/psum | solution.py:19
  134.4 2.0 %broadcast_bitcast_fusion = bf16[64,64,2,64]{3,2,1,0:T(2,128)(2,1)S(1)} fusion(bf16[2,64,64]{2,0,1:T(2,128)(2,1)S(1)} %copy.52), kind=kLoop, calls=%fused_computation.82 | loop fusion | bytes 1064960
  136.4 2.3 %reshape.178 = bf16[64,2,4096]{2,1,0:T(2,128)(2,1)} reshape(bf16[64,64,2,64]{3,2,1,0:T(2,128)(2,1)S(1)} %broadcast_bitcast_fusion) | data formatting | bytes 2097152
  138.7 7.5 %all-to-all-start.2 = ((bf16[64,2,4096]{2,1,0:T(2,128)(2,1)}), bf16[64,2,4096]{2,1,0:T(2,128)(2,1)S(1)}, u32[]{:S(2)}, u32[]{:S(2)}) async-start(bf16[64,2,4096]{2,1,0:T(2,128)(2,1)} %reshape.178), calls=%async_computation.2 | async-start | bytes 2097152 | tf_op jit(solution)/shard_map/all_to_all | solution.py:31
  146.3 4.9 %fusion.8 = f32[1,64,128,64]{2,3,1,0:T(8,128)S(1)} fusion(f32[128,64,64]{0,2,1:T(8,128)} %fusion.2, f32[64]{0:T(128)S(1)} %get-tuple-element.10, f32[64]{0:T(128)S(1)} %get-tuple-element.11), kind=kOutput, calls=%fused_computation.13 | convolution fusion | flops 402665472 | bytes 4194816 | tf_op jit(solution)/shard_map/ka,ckl,lb->cab/dot_general | solution.py:59
  151.1 2.7 %copy.45 = f32[1,64,128,64]{3,2,1,0:T(8,128)} copy(f32[1,64,128,64]{2,3,1,0:T(8,128)S(1)} %fusion.8) | data formatting | bytes 4194304 | tf_op jit(solution)/shard_map/transpose | solution.py:55
  153.8 3.5 %reshape.172 = f32[1,64,8192]{2,1,0:T(8,128)S(1)} reshape(f32[1,64,128,64]{3,2,1,0:T(8,128)} %copy.45) | data formatting | bytes 4194304 | tf_op jit(solution)/shard_map/reshape | solution.py:55
  157.3 2.9 %subtract_convert_fusion = bf16[1,64,8192]{2,1,0:T(8,128)(2,1)} fusion(f32[1,64,8192]{2,1,0:T(8,128)S(1)} %reshape.172, bf16[1,64,8192]{2,1,0:T(8,128)(2,1)} %param.3, bf16[1,64,8192]{2,1,0:T(8,128)(2,1)} %param.4), kind=kLoop, calls=%fused_computation.7 | loop fusion | flops 3145728 | bytes 5242880 | tf_op jit(solution)/shard_map/convert_element_type | solution.py:95
  160.2 15.7 %all-to-all-done.2 = bf16[64,2,4096]{2,1,0:T(2,128)(2,1)S(1)} async-done(((bf16[64,2,4096]{2,1,0:T(2,128)(2,1)}), bf16[64,2,4096]{2,1,0:T(2,128)(2,1)S(1)}, u32[]{:S(2)}, u32[]{:S(2)}) %all-to-all-start.2) | async-done | bytes 1048608 | tf_op jit(solution)/shard_map/all_to_all | solution.py:31
  175.9 1.3 reshape.179
  177.3 0.6 copy.53
  177.8 1.4 copy.54
  179.2 2.5 %reshape.174 = bf16[64,8192]{1,0:T(8,128)(2,1)} reshape(bf16[1,64,128,64]{3,2,1,0:T(8,128)(2,1)S(1)} %copy.54) | data formatting | bytes 2097152 | tf_op jit(solution)/shard_map/reshape | solution.py:55
  (6 shorter events, 0.1 us)
Async XLA Ops:
  5.5 3.5 %copy-start.1 = (s32[1,1,128,32]{2,3,1,0:T(8,128)S(1)}, s32[1,1,128,32]{2,3,1,0:T(8,128)}, u32[]{:S(2)}) copy-start(s32[1,1,128,32]{2,3,1,0:T(8,128)} %param.5) | copy-start | bytes 49156
  18.4 2.2 %copy-start = (f32[128,64,64]{0,2,1:T(8,128)S(1)}, f32[128,64,64]{0,2,1:T(8,128)}, u32[]{:S(2)}) copy-start(f32[128,64,64]{0,2,1:T(8,128)} %copy.40) | copy-start | bytes 6291460
  36.7 27.8 %all-to-all-start.1 = ((bf16[64,2,32]{2,1,0:T(2,128)(2,1)}), bf16[64,2,32]{2,1,0:T(2,128)(2,1)S(1)}, u32[]{:S(2)}, u32[]{:S(2)}) async-start(bf16[64,2,32]{2,1,0:T(2,128)(2,1)} %bitcast.10), calls=%async_computation.1 | async-start | bytes 65536 | tf_op jit(solution)/shard_map/all_to_all | solution.py:106
  64.4 17.0 %all-to-all-start = ((s32[64,2,32]{2,1,0:T(2,128)}), s32[64,2,32]{2,1,0:T(2,128)S(1)}, u32[]{:S(2)}, u32[]{:S(2)}) async-start(s32[64,2,32]{2,1,0:T(2,128)} %bitcast.8), calls=%async_computation | async-start | bytes 131072 | tf_op jit(solution)/shard_map/all_to_all | solution.py:107
  138.7 37.2 %all-to-all-start.2 = ((bf16[64,2,4096]{2,1,0:T(2,128)(2,1)}), bf16[64,2,4096]{2,1,0:T(2,128)(2,1)S(1)}, u32[]{:S(2)}, u32[]{:S(2)}) async-start(bf16[64,2,4096]{2,1,0:T(2,128)(2,1)} %reshape.178), calls=%async_computation.2 | async-start | bytes 2097152 | tf_op jit(solution)/shard_map/all_to_all | solution.py:31
where the time goes:
time: 182 us
  blocking collectives  45.6 us (25%)
  waiting for transfers between devices  37.3 us (20%)
  local copies, waits for them, and re-layouts  34.4 us (19%)
  starting transfers between devices  29.8 us (16%)
  matrix products  28.3 us (16%)
  other arithmetic  4.81 us (3%)
    psum x4, blocking collectives, one_axis_at_a_time(): value = lax.psum(value, axis)  45.6 us
    all_to_all x1, starting transfers between devices, local(): lax.all_to_all(outgoing[0], DP, split_axis=0, concat_axis=0, tiled=True)  16.8 us
    all_to_all x1, waiting for transfers between devices, from_everyone(): return lax.all_to_all(copies, axis, split_axis=0, concat_axis=0, tiled=True)  15.7 us
    all_to_all x1, waiting for transfers between devices, local(): lax.all_to_all(outgoing[1], DP, split_axis=0, concat_axis=0, tiled=True)  11.4 us
    dot_general x4, matrix products, inverse(): jnp.einsum('ka,ckl,lb->cab', cosines, spectra, cosines, precision=lax.Pre...  11 us
    all_to_all x1, waiting for transfers between devices, local(): lax.all_to_all(outgoing[0], DP, split_axis=0, concat_axis=0, tiled=True)  10.2 us
    all_to_all x1, starting transfers between devices, from_everyone(): return lax.all_to_all(copies, axis, split_axis=0, concat_axis=0, tiled=True)  7.53 us
    dot_general x2, matrix products, local(): jnp.einsum('ka,cab,lb->ckl', cosines, to_spans(renewed, block_edge), cosi...  6.9 us
  transfers between devices with their start and end apart: 3, of which 3 were waited for; matrix products, arithmetic and copies ran while one was open for 8% of the time, Pallas kernels for 0%

commit v1 on v0

v1 whole, which is shorter than its diff:
```python
import functools

import jax
import jax.numpy as jnp
import numpy as np
from jax import lax
from jax.experimental import pallas as pl
from jax.experimental.pallas import tpu as pltpu
from jax.sharding import PartitionSpec as P

MESH = pl.DeviceIdType.MESH
BLOCK = 64
TOPK = 32
CHUNK = 256
RING = 8
GROUP = 4
EPSILON = 1e-06
DECAY = 0.999
F32 = jnp.float32
BF16 = jnp.bfloat16


def basis():
    frequency = np.arange(BLOCK, dtype=np.float64)[:, None]
    position = np.arange(BLOCK, dtype=np.float64)[None, :]
    waves = np.cos(np.pi * (2.0 * position + 1.0) * frequency / (2.0 * BLOCK))
    return waves * np.where(frequency == 0.0, np.sqrt(1.0 / BLOCK), np.sqrt(2.0 / BLOCK))


def halves(array):
    array = array.astype(np.float32)
    high = array.astype(BF16)
    low = (array - high.astype(np.float32)).astype(BF16)
    return high, low


def right_constants(matrix):
    return np.stack([np.kron(np.eye(4), half.astype(np.float32)).astype(BF16) for half in halves(matrix)])


def left_constants(matrix):
    high, low = halves(matrix)
    return np.concatenate([high, high, low, low], axis=1)


def dot(a, b):
    return jnp.dot(a, b, preferred_element_type=F32)


def dot_nt(a, b):
    return lax.dot_general(a, b, (((1,), (1,)), ((), ())), preferred_element_type=F32)


def split(x):
    high = x.astype(BF16)
    return high, (x - high.astype(F32)).astype(BF16)


def left(constants, y):
    high, low = split(y)
    return dot(constants, jnp.concatenate([high, low, high, low], axis=0))


def right(x, high_constants, low_constants):
    high, low = split(x)
    return dot(high, high_constants) + dot(low, high_constants) + dot(high, low_constants)


def iota(shape, dim):
    return lax.broadcasted_iota(jnp.int32, shape, dim)


def kernel(
    total_count,
    g_hbm,
    m_hbm,
    idx_ref,
    fwd_right,
    inv_right,
    fwd_left,
    inv_left,
    nm_hbm,
    up_hbm,
    g_ref,
    m_ref,
    nm_ref,
    up_ref,
    s_ref,
    ob_ref,
    oa_ref,
    turned_ref,
    il_ref,
    msg_ref,
    recv_ref,
    land_ref,
    ex_ref,
    ey_ref,
    ez_ref,
    in_sem,
    out_sem,
    msg_send,
    msg_recv,
    land_send,
    land_recv,
    e_send,
    e_recv,
):
    me = lax.axis_index("dp")
    tensor = lax.axis_index("tensor")
    z, y = me // RING, lax.rem(me, RING)
    replicas = RING * RING
    chunks = s_ref.shape[0]
    groups = chunks // GROUP
    wide = GROUP * CHUNK

    def group_columns(i):
        return pl.ds(pl.multiple_of(i * wide, wide), wide)

    def load(i, which):
        hbm, ref = ((g_hbm, g_ref), (m_hbm, m_ref))[which]
        return pltpu.make_async_copy(
            hbm.at[0, :, group_columns(i)], ref.at[:, group_columns(i)], in_sem.at[which, i]
        )

    for i in range(groups):
        load(i, 0).start()
        load(i, 1).start()

    barrier = pltpu.get_barrier_semaphore()

    def greet_dp(k, carry):
        pl.semaphore_signal(barrier, inc=1, device_id={"dp": lax.rem(me + k, replicas)}, device_id_type=MESH)
        return carry

    def greet_tensor(k, carry):
        pl.semaphore_signal(barrier, inc=1, device_id={"tensor": lax.rem(tensor + k, RING)}, device_id_type=MESH)
        return carry

    lax.fori_loop(1, replicas, greet_dp, 0)
    lax.fori_loop(1, RING, greet_tensor, 0)

    turned_ref[...] = jnp.transpose(idx_ref[...])
    il_ref[...] = jnp.concatenate(
        [turned_ref[pl.ds(k, chunks, stride=4), :] for k in range(4)], axis=1
    )
    lane_span = iota((1, 128), 1) // TOPK

    def renewed(c):
        columns = pl.ds(pl.multiple_of(c * CHUNK, CHUNK), CHUNK)
        return DECAY * m_ref[:, columns].astype(F32) + g_ref[:, columns].astype(F32)

    def compress(i, carry):
        load(i, 0).wait()
        load(i, 1).wait()
        pieces = [split(renewed(i * GROUP + c)) for c in range(GROUP)]
        high = jnp.concatenate([p[0] for p in pieces], axis=0)
        low = jnp.concatenate([p[1] for p in pieces], axis=0)
        half = dot(high, fwd_right[0]) + dot(low, fwd_right[0]) + dot(high, fwd_right[1])
        for c in range(GROUP):
            chunk = i * GROUP + c
            spectrum = left(fwd_left[...], half[c * BLOCK : (c + 1) * BLOCK])
            s_ref[chunk] = spectrum
            ids = il_ref[pl.ds(chunk, 1), :]
            row_hit = iota((BLOCK, 128), 0) == ids // BLOCK
            col_hit = iota((CHUNK, 128), 0) == lax.rem(ids, BLOCK) + BLOCK * lane_span
            col_ones = jnp.where(col_hit, 1.0, 0.0).astype(BF16)
            ob_ref[chunk] = col_ones
            oa_ref[chunk] = jnp.where(row_hit, 1.0, 0.0).astype(BF16)
            by_column = dot(spectrum.astype(BF16), col_ones)
            msg_ref[chunk, 0:1, :] = jnp.sum(jnp.where(row_hit, by_column, 0.0), axis=0, keepdims=True)
            msg_ref[chunk, 1:2, :] = ids.astype(F32)
        return carry

    lax.fori_loop(0, groups, compress, 0)

    pl.semaphore_wait(barrier, replicas - 1 + RING - 1)

    def send_values(k, carry):
        peer = lax.rem(me + k, replicas)
        pltpu.make_async_remote_copy(
            src_ref=msg_ref.at[peer // 2],
            dst_ref=recv_ref.at[me],
            send_sem=msg_send,
            recv_sem=msg_recv,
            device_id={"dp": peer},
            device_id_type=MESH,
        ).start()
        return carry

    lax.fori_loop(1, replicas, send_values, 0)

    def store(i):
        return pltpu.make_async_copy(
            nm_ref.at[:, group_columns(i)], nm_hbm.at[0, :, group_columns(i)], out_sem.at[0, i]
        )

    def remove(i, carry):
        rows = []
        for c in range(GROUP):
            chunk = i * GROUP + c
            marker = dot_nt(oa_ref[chunk], ob_ref[chunk])
            rows.append(split(left(inv_left[...], s_ref[chunk] * marker)))
        high = jnp.concatenate([r[0] for r in rows], axis=0)
        low = jnp.concatenate([r[1] for r in rows], axis=0)
        restored = dot(high, inv_right[0]) + dot(low, inv_right[0]) + dot(high, inv_right[1])
        for c in range(GROUP):
            chunk = i * GROUP + c
            columns = pl.ds(pl.multiple_of(chunk * CHUNK, CHUNK), CHUNK)
            nm_ref[:, columns] = (renewed(chunk) - restored[c * BLOCK : (c + 1) * BLOCK]).astype(BF16)
        store(i).start()
        return carry

    lax.fori_loop(0, groups, remove, 0)

    others = recv_ref.at[pl.ds(0, replicas - 1)]
    pltpu.make_async_copy(others, others, msg_recv).wait()
    recv_ref[me] = msg_ref[me // 2]

    odd = lax.rem(me, 2)
    lane = iota((replicas // 2, 128), 1)

    def mine(array):
        array = jnp.where(odd == 0, array, pltpu.roll(array, 64, 1))
        return jnp.where(lane < 64, array[: replicas // 2], pltpu.roll(array[replicas // 2 :], 64, 1))

    got_values = mine(recv_ref[:, 0, :])
    got_ids = mine(recv_ref[:, 1, :]).astype(jnp.int32)
    got_rows = got_ids // BLOCK
    got_cols = lax.rem(got_ids, BLOCK) + BLOCK * lax.rem(lane // TOPK, 2)
    combined = jnp.zeros((BLOCK, 128), F32)
    for r in range(0, replicas // 2, 2):
        rows, cols = [], []
        for k in (r, r + 1):
            rows.append(
                jnp.where(iota((BLOCK, 128), 0) == got_rows[k : k + 1], got_values[k : k + 1], 0.0).astype(BF16)
            )
            cols.append(jnp.where(iota((128, 128), 0) == got_cols[k : k + 1], 1.0, 0.0).astype(BF16))
        combined += dot_nt(jnp.concatenate(rows, axis=1), jnp.concatenate(cols, axis=1))
    decoded = left(inv_left[...], right(combined, inv_right[0, :128, :128], inv_right[1, :128, :128]))
    rounded = decoded.astype(BF16)
    half_rows = BLOCK // 2
    land_ref[0, me] = rounded[:half_rows]
    land_ref[1, me] = rounded[half_rows:]

    energy_refs = (ex_ref, ey_ref, ez_ref)
    energy_places = (tensor, y, z)

    def energy_target(stage, place):
        if stage == 0:
            return {"tensor": place}
        return {"dp": z * RING + place if stage == 1 else place * RING + y}

    def send_energy(stage, row):
        ref, place = energy_refs[stage], energy_places[stage]
        ref[place] = row

        def send(k, carry):
            peer = lax.rem(place + k, RING)
            pltpu.make_async_remote_copy(
                src_ref=ref.at[place],
                dst_ref=ref.at[place],
                send_sem=e_send.at[stage],
                recv_sem=e_recv.at[stage],
                device_id=energy_target(stage, peer),
                device_id_type=MESH,
            ).start()
            return carry

        lax.fori_loop(1, RING, send, 0)

    def take_energy(stage):
        ref = energy_refs[stage]
        rest = ref.at[pl.ds(0, RING - 1)]
        pltpu.make_async_copy(rest, rest, e_recv.at[stage]).wait()
        pltpu.make_async_copy(rest, rest, e_send.at[stage]).wait()
        row = ref[0]
        for k in range(1, RING):
            row = row + ref[k]
        return row

    send_energy(0, jnp.sum(decoded * decoded, axis=0, keepdims=True))

    along = ((y, z), (z, y))

    def place_of(h, a, b):
        a, b = lax.rem(a + 2 * RING, RING), lax.rem(b + 2 * RING, RING)
        return b * RING + a if h == 0 else a * RING + b

    def send_item(h, item, target):
        pltpu.make_async_remote_copy(
            src_ref=land_ref.at[h, item],
            dst_ref=land_ref.at[h, item],
            send_sem=land_send.at[h],
            recv_sem=land_recv.at[h, item],
            device_id={"dp": target},
            device_id_type=MESH,
        ).start()

    def wait_item(h, item):
        ref = land_ref.at[h, item]
        pltpu.make_async_copy(ref, ref, land_recv.at[h, item]).wait()

    def nearest(i):
        return ((i + 1) // 2) * (2 * lax.rem(i, 2) - 1)

    def first_sends(i, carry):
        for h in range(2):
            a, b = along[h]
            send_item(h, me, place_of(h, a + nearest(RING - i), b))
        return carry

    lax.fori_loop(1, RING, first_sends, 0)

    def spread(h, item):
        a, b = along[h]
        for step in (2, -2, 1, -1):
            send_item(h, item, place_of(h, a, b + step))

    for h in range(2):
        spread(h, me)

    def second_sends(i, carry):
        for h in range(2):
            a, b = along[h]
            item = place_of(h, a + nearest(i), b)
            wait_item(h, item)
            spread(h, item)
        return carry

    lax.fori_loop(1, 4, second_sends, 0)
    send_energy(1, take_energy(0))
    lax.fori_loop(4, RING, second_sends, 0)

    def third_sends(i, carry):
        for h in range(2):
            a, b = along[h]
            other = a + jnp.where(i == 0, 0, nearest(i))
            other = lax.rem(other + RING, RING)
            for step in (2, -2):
                item = place_of(h, other, b - step)
                wait_item(h, item)
                send_item(h, item, place_of(h, a, b + step // 2))
            sign = 1 - 2 * lax.rem(other, 2)
            send_item(h, place_of(h, other, b - 2 * sign), place_of(h, a, b + 2 * sign))
        return carry

    lax.fori_loop(0, 4, third_sends, 0)
    send_energy(2, take_energy(1))
    lax.fori_loop(4, RING, third_sends, 0)

    energy = jnp.sum(take_energy(2), axis=1, keepdims=True)
    scale = 1.0 / jnp.sqrt(energy / total_count + EPSILON)

    def last_waits(i, carry):
        for h in range(2):
            b = along[h][1]
            for step in (1, -1, 3, -3, 4):
                wait_item(h, place_of(h, i, b + step))
        return carry

    lax.fori_loop(0, RING, last_waits, 0)

    def put(i):
        return pltpu.make_async_copy(up_ref.at[:, group_columns(i)], up_hbm.at[:, group_columns(i)], out_sem.at[1, i])

    per_group = wide // 128

    def finish(i, carry):
        for k in range(per_group):
            item = i * per_group + k
            columns = pl.ds(pl.multiple_of(item * 128, 128), 128)
            for h in range(2):
                up_ref[h * half_rows : (h + 1) * half_rows, columns] = (
                    land_ref[h, item].astype(F32) * scale
                ).astype(BF16)
        put(i).start()
        return carry

    lax.fori_loop(0, groups, finish, 0)

    pltpu.make_async_copy(others, others, msg_send).wait()
    for h in range(2):
        rest = land_ref.at[h, pl.ds(0, replicas - 1)]
        pltpu.make_async_copy(rest, rest, land_send.at[h]).wait()
    for i in range(groups):
        store(i).wait()
        put(i).wait()


def local(total_count, gradient, momentum, indices):
    _, height, columns = gradient.shape
    chunks = columns // CHUNK
    groups = chunks // GROUP
    replicas = RING * RING
    cosines = basis()
    anywhere = pl.BlockSpec(memory_space=pl.ANY)
    vmem = pl.BlockSpec(memory_space=pltpu.VMEM)
    dma = pltpu.SemaphoreType.DMA
    return pl.pallas_call(
        functools.partial(kernel, total_count),
        out_shape=(
            jax.ShapeDtypeStruct((1, height, columns), BF16),
            jax.ShapeDtypeStruct((height, columns), BF16),
        ),
        in_specs=[anywhere, anywhere, vmem, vmem, vmem, vmem, vmem],
        out_specs=(anywhere, anywhere),
        scratch_shapes=[
            pltpu.VMEM((height, columns), BF16),
            pltpu.VMEM((height, columns), BF16),
            pltpu.VMEM((height, columns), BF16),
            pltpu.VMEM((height, columns), BF16),
            pltpu.VMEM((chunks, BLOCK, CHUNK), F32),
            pltpu.VMEM((chunks, CHUNK, 128), BF16),
            pltpu.VMEM((chunks, BLOCK, 128), BF16),
            pltpu.VMEM((chunks * 4, TOPK), jnp.int32),
            pltpu.VMEM((chunks, 128), jnp.int32),
            pltpu.VMEM((chunks, 2, 128), F32),
            pltpu.VMEM((replicas, 2, 128), F32),
            pltpu.VMEM((2, replicas, BLOCK // 2, 128), BF16),
            pltpu.VMEM((RING, 1, 128), F32),
            pltpu.VMEM((RING, 1, 128), F32),
            pltpu.VMEM((RING, 1, 128), F32),
            dma((2, groups)),
            dma((2, groups)),
            dma,
            dma,
            dma((2,)),
            dma((2, replicas)),
            dma((3,)),
            dma((3,)),
        ],
        compiler_params=pltpu.CompilerParams(collective_id=0, has_side_effects=True),
        name="demo_step",
    )(
        gradient,
        momentum,
        jnp.transpose(indices.reshape(columns // BLOCK, TOPK)),
        right_constants(cosines.T),
        right_constants(cosines),
        left_constants(cosines),
        left_constants(cosines.T),
    )


def solution(mesh):
    def whole(gradient, momentum, indices):
        rows, columns = gradient.shape[1:]
        return jax.shard_map(
            functools.partial(local, float(rows * columns)),
            mesh=mesh,
            in_specs=(P("dp", "tensor", None), P("dp", "tensor", None), P("dp", "tensor", None, None)),
            out_specs=(P("dp", "tensor", None), P("tensor", None)),
            check_vma=False,
        )(gradient, momentum, indices)

    return whole
```

time: 182 us -> 49.9 us (0.27)
  the two profiles are of different devices: /device:TPU:8 before, /device:TPU:2 now
where the time goes in v1:
time: 49.9 us; the launch traced here: 49.7 us
  Pallas kernels  45.7 us (92%)
  local copies, waits for them, and re-layouts  3.32 us (7%)
  between operations  0.65 us (1%)
    pallas_call x1, Pallas kernels, local(): pl.pallas_call(functools.partial(kernel, total_count), out_shape=(jax.Sha...  45.7 us
    unnamed x4, local copies, waits for them, and re-layouts  3.32 us

profile of v1, /device:TPU:2, one launch (start us, length us, event | category | flops | bytes accessed | tf_op | source)
XLA Modules:
  0.0 49.7 jit_solution(16645548133537032760)
XLA Ops:
  0.6 45.7 %demo_step.1 = (bf16[1,64,8192]{2,1,0:T(8,128)(2,1)}, bf16[64,8192]{1,0:T(8,128)(2,1)}) custom-call(bf16[1,64,8192]{2,1,0:T(8,128)(2,1)} %g_hbm.1, bf16[1,64,8192]{2,1,0:T(8,128)(2,1)} %m_hbm.1, s32[32,128]{1,0:T(8,128)} %bitcast.3, bf16[2,256,256]{2,1,0:T(8,128)(2,1)} %constant.8.clone.fwd_right, bf16[2,256,256]{2,1,0:T(8,128)(2,1)} %constant.9.clone.inv_right, ...), custom_call_target="tpu_custom_call" | custom-call | tf_op jit(solution)/shard_map/demo_step/pallas_call | solution.py:399
  46.4 0.0 copy-start
  46.4 2.4 %copy.11 = bf16[1,64,8192]{2,1,0:T(8,128)(2,1)} copy(bf16[1,64,8192]{2,1,0:T(8,128)(2,1)} %get-tuple-element.4) | data formatting | bytes 2097152
  48.7 0.0 copy-done
  48.7 1.0 %copy.12 = bf16[64,8192]{1,0:T(8,128)(2,1)} copy(bf16[64,8192]{1,0:T(8,128)(2,1)S(1)} %copy-done) | data formatting | bytes 2097152
Async XLA Ops:
  46.4 2.4 %copy-start = (bf16[64,8192]{1,0:T(8,128)(2,1)S(1)}, bf16[64,8192]{1,0:T(8,128)(2,1)}, u32[]{:S(2)}) copy-start(bf16[64,8192]{1,0:T(8,128)(2,1)} %get-tuple-element.5) | copy-start | bytes 3145732

commit v2 on v1

--- a/solution.py
+++ b/solution.py
@@ -13,7 +13,7 @@
 TOPK = 32
 CHUNK = 256
 RING = 8
-GROUP = 4
+GROUP = 8
 EPSILON = 1e-06
 DECAY = 0.999
 F32 = jnp.float32
@@ -38,6 +38,17 @@
     return np.stack([np.kron(np.eye(4), half.astype(np.float32)).astype(BF16) for half in halves(matrix)])
 
 
+def pair_constants(matrix):
+    pair = np.concatenate([np.kron(np.eye(2), half.astype(np.float32)).astype(BF16) for half in halves(matrix)], axis=1)
+    return np.concatenate([pair, pair], axis=0)
+
+
+def entry_constants(matrix):
+    return np.concatenate(
+        [np.concatenate(pair, axis=1) for pair in zip(halves(DECAY * matrix), halves(matrix))], axis=0
+    )
+
+
 def left_constants(matrix):
     high, low = halves(matrix)
     return np.concatenate([high, high, low, low], axis=1)
@@ -74,17 +85,21 @@
     total_count,
     g_hbm,
     m_hbm,
+    idx_hbm,
+    fwd_pair_hbm,
+    inv_right_hbm,
+    entry_hbm,
+    inv_left_hbm,
+    nm_ref,
+    up_ref,
     idx_ref,
-    fwd_right,
+    fwd_pair,
     inv_right,
-    fwd_left,
+    entry,
     inv_left,
-    nm_hbm,
-    up_hbm,
     g_ref,
     m_ref,
-    nm_ref,
-    up_ref,
+    y_ref,
     s_ref,
     ob_ref,
     oa_ref,
@@ -96,8 +111,8 @@
     ex_ref,
     ey_ref,
     ez_ref,
+    const_sem,
     in_sem,
-    out_sem,
     msg_send,
     msg_recv,
     land_send,
@@ -109,7 +124,7 @@
     tensor = lax.axis_index("tensor")
     z, y = me // RING, lax.rem(me, RING)
     replicas = RING * RING
-    chunks = s_ref.shape[0]
+    chunks = ob_ref.shape[0]
     groups = chunks // GROUP
     wide = GROUP * CHUNK
 
@@ -122,56 +137,99 @@
             hbm.at[0, :, group_columns(i)], ref.at[:, group_columns(i)], in_sem.at[which, i]
         )
 
+    barrier = pltpu.get_barrier_semaphore()
+
+    def greet_dp(k, carry):
+        pl.semaphore_signal(barrier, inc=1, device_id={"dp": lax.rem(me + k, replicas)}, device_id_type=MESH)
+        return carry
+
+    def greet_tensor(k, carry):
+        pl.semaphore_signal(barrier, inc=1, device_id={"tensor": lax.rem(tensor + k, RING)}, device_id_type=MESH)
+        return carry
+
+    lax.fori_loop(1, replicas, greet_dp, 0)
+    lax.fori_loop(1, RING, greet_tensor, 0)
+
+    small = [
+        pltpu.make_async_copy(hbm, ref, const_sem.at[i])
+        for i, (hbm, ref) in enumerate(
+            [
+                (idx_hbm, idx_ref),
+                (entry_hbm, entry),
+                (fwd_pair_hbm, fwd_pair),
+                (inv_right_hbm, inv_right),
+                (inv_left_hbm, inv_left),
+            ]
+        )
+    ]
+    for copy in small[:3]:
+        copy.start()
     for i in range(groups):
         load(i, 0).start()
         load(i, 1).start()
-
-    barrier = pltpu.get_barrier_semaphore()
-
-    def greet_dp(k, carry):
-        pl.semaphore_signal(barrier, inc=1, device_id={"dp": lax.rem(me + k, replicas)}, device_id_type=MESH)
-        return carry
-
-    def greet_tensor(k, carry):
-        pl.semaphore_signal(barrier, inc=1, device_id={"tensor": lax.rem(tensor + k, RING)}, device_id_type=MESH)
-        return carry
-
-    lax.fori_loop(1, replicas, greet_dp, 0)
-    lax.fori_loop(1, RING, greet_tensor, 0)
-
+    for copy in small[3:]:
+        copy.start()
+
+    small[0].wait()
     turned_ref[...] = jnp.transpose(idx_ref[...])
     il_ref[...] = jnp.concatenate(
         [turned_ref[pl.ds(k, chunks, stride=4), :] for k in range(4)], axis=1
     )
     lane_span = iota((1, 128), 1) // TOPK
 
+    def mark(chunk, carry):
+        ids = il_ref[pl.ds(chunk, 1), :]
+        row_hit = iota((BLOCK, 128), 0) == ids // BLOCK
+        col_hit = iota((CHUNK, 128), 0) == lax.rem(ids, BLOCK) + BLOCK * lane_span
+        ob_ref[chunk] = jnp.where(col_hit, 1.0, 0.0).astype(BF16)
+        oa_ref[chunk] = jnp.where(row_hit, 1.0, 0.0).astype(BF16)
+        msg_ref[chunk, 1:2, :] = ids.astype(F32)
+        return carry
+
+    lax.fori_loop(0, chunks, mark, 0, unroll=2)
+
     def renewed(c):
         columns = pl.ds(pl.multiple_of(c * CHUNK, CHUNK), CHUNK)
         return DECAY * m_ref[:, columns].astype(F32) + g_ref[:, columns].astype(F32)
 
-    def compress(i, carry):
+    small[1].wait()
+    small[2].wait()
+
+    def rows_first(i):
         load(i, 0).wait()
         load(i, 1).wait()
-        pieces = [split(renewed(i * GROUP + c)) for c in range(GROUP)]
-        high = jnp.concatenate([p[0] for p in pieces], axis=0)
-        low = jnp.concatenate([p[1] for p in pieces], axis=0)
-        half = dot(high, fwd_right[0]) + dot(low, fwd_right[0]) + dot(high, fwd_right[1])
-        for c in range(GROUP):
-            chunk = i * GROUP + c
-            spectrum = left(fwd_left[...], half[c * BLOCK : (c + 1) * BLOCK])
-            s_ref[chunk] = spectrum
-            ids = il_ref[pl.ds(chunk, 1), :]
-            row_hit = iota((BLOCK, 128), 0) == ids // BLOCK
-            col_hit = iota((CHUNK, 128), 0) == lax.rem(ids, BLOCK) + BLOCK * lane_span
-            col_ones = jnp.where(col_hit, 1.0, 0.0).astype(BF16)
-            ob_ref[chunk] = col_ones
-            oa_ref[chunk] = jnp.where(row_hit, 1.0, 0.0).astype(BF16)
-            by_column = dot(spectrum.astype(BF16), col_ones)
-            msg_ref[chunk, 0:1, :] = jnp.sum(jnp.where(row_hit, by_column, 0.0), axis=0, keepdims=True)
-            msg_ref[chunk, 1:2, :] = ids.astype(F32)
-        return carry
-
-    lax.fori_loop(0, groups, compress, 0)
+        for c in range(i * GROUP, (i + 1) * GROUP):
+            columns = slice(c * CHUNK, (c + 1) * CHUNK)
+            both = dot(entry[...], jnp.concatenate([m_ref[:, columns], g_ref[:, columns]], axis=0))
+            high, low = split(both[:BLOCK] + both[BLOCK:])
+            for k in range(2):
+                rows = slice((2 * c + k) * BLOCK, (2 * c + k + 1) * BLOCK)
+                y_ref[rows, :128] = high[:, k * 128 : (k + 1) * 128]
+                y_ref[rows, 128:] = low[:, k * 128 : (k + 1) * 128]
+
+    def columns_next(i):
+        rows = slice(i * GROUP * 2 * BLOCK, (i + 1) * GROUP * 2 * BLOCK)
+        both = dot(y_ref[rows, :], fwd_pair[...])
+        s_ref[rows, :] = both[:, :128] + both[:, 128:]
+
+    def spectrum_of(c):
+        start = c * 2 * BLOCK
+        return jnp.concatenate([s_ref[pl.ds(start, BLOCK), :], s_ref[pl.ds(start + BLOCK, BLOCK), :]], axis=1)
+
+    def pick(i):
+        for c in range(i * GROUP, (i + 1) * GROUP):
+            by_column = dot(spectrum_of(c).astype(BF16), ob_ref[c])
+            msg_ref[c, 0:1, :] = jnp.sum(by_column * oa_ref[c].astype(F32), axis=0, keepdims=True)
+
+    for i in range(groups + 2):
+        if i >= 2:
+            pick(i - 2)
+        if 1 <= i <= groups:
+            columns_next(i - 1)
+        if i < groups:
+            rows_first(i)
+    small[3].wait()
+    small[4].wait()
 
     pl.semaphore_wait(barrier, replicas - 1 + RING - 1)
 
@@ -189,17 +247,12 @@
 
     lax.fori_loop(1, replicas, send_values, 0)
 
-    def store(i):
-        return pltpu.make_async_copy(
-            nm_ref.at[:, group_columns(i)], nm_hbm.at[0, :, group_columns(i)], out_sem.at[0, i]
-        )
-
     def remove(i, carry):
         rows = []
         for c in range(GROUP):
             chunk = i * GROUP + c
             marker = dot_nt(oa_ref[chunk], ob_ref[chunk])
-            rows.append(split(left(inv_left[...], s_ref[chunk] * marker)))
+            rows.append(split(left(inv_left[...], spectrum_of(chunk) * marker)))
         high = jnp.concatenate([r[0] for r in rows], axis=0)
         low = jnp.concatenate([r[1] for r in rows], axis=0)
         restored = dot(high, inv_right[0]) + dot(low, inv_right[0]) + dot(high, inv_right[1])
@@ -207,7 +260,6 @@
             chunk = i * GROUP + c
             columns = pl.ds(pl.multiple_of(chunk * CHUNK, CHUNK), CHUNK)
             nm_ref[:, columns] = (renewed(chunk) - restored[c * BLOCK : (c + 1) * BLOCK]).astype(BF16)
-        store(i).start()
         return carry
 
     lax.fori_loop(0, groups, remove, 0)
@@ -360,9 +412,6 @@
 
     lax.fori_loop(0, RING, last_waits, 0)
 
-    def put(i):
-        return pltpu.make_async_copy(up_ref.at[:, group_columns(i)], up_hbm.at[:, group_columns(i)], out_sem.at[1, i])
-
     per_group = wide // 128
 
     def finish(i, carry):
@@ -373,7 +422,6 @@
                 up_ref[h * half_rows : (h + 1) * half_rows, columns] = (
                     land_ref[h, item].astype(F32) * scale
                 ).astype(BF16)
-        put(i).start()
         return carry
 
     lax.fori_loop(0, groups, finish, 0)
@@ -382,9 +430,6 @@
     for h in range(2):
         rest = land_ref.at[h, pl.ds(0, replicas - 1)]
         pltpu.make_async_copy(rest, rest, land_send.at[h]).wait()
-    for i in range(groups):
-        store(i).wait()
-        put(i).wait()
 
 
 def local(total_count, gradient, momentum, indices):
@@ -394,22 +439,25 @@
     replicas = RING * RING
     cosines = basis()
     anywhere = pl.BlockSpec(memory_space=pl.ANY)
-    vmem = pl.BlockSpec(memory_space=pltpu.VMEM)
     dma = pltpu.SemaphoreType.DMA
-    return pl.pallas_call(
+    nm, up = pl.pallas_call(
         functools.partial(kernel, total_count),
         out_shape=(
-            jax.ShapeDtypeStruct((1, height, columns), BF16),
-            jax.ShapeDtypeStruct((height, columns), BF16),
-        ),
-        in_specs=[anywhere, anywhere, vmem, vmem, vmem, vmem, vmem],
-        out_specs=(anywhere, anywhere),
-        scratch_shapes=[
             pltpu.VMEM((height, columns), BF16),
             pltpu.VMEM((height, columns), BF16),
+        ),
+        in_specs=[anywhere] * 7,
+        out_specs=(pl.BlockSpec(memory_space=pltpu.VMEM),) * 2,
+        scratch_shapes=[
+            pltpu.VMEM((TOPK, columns // BLOCK), jnp.int32),
+            pltpu.VMEM((256, 256), BF16),
+            pltpu.VMEM((2, 256, 256), BF16),
+            pltpu.VMEM((128, 128), BF16),
+            pltpu.VMEM((BLOCK, 256), BF16),
             pltpu.VMEM((height, columns), BF16),
             pltpu.VMEM((height, columns), BF16),
-            pltpu.VMEM((chunks, BLOCK, CHUNK), F32),
+            pltpu.VMEM((chunks * 2 * BLOCK, 256), BF16),
+            pltpu.VMEM((chunks * 2 * BLOCK, 128), F32),
             pltpu.VMEM((chunks, CHUNK, 128), BF16),
             pltpu.VMEM((chunks, BLOCK, 128), BF16),
             pltpu.VMEM((chunks * 4, TOPK), jnp.int32),
@@ -420,7 +468,7 @@
             pltpu.VMEM((RING, 1, 128), F32),
             pltpu.VMEM((RING, 1, 128), F32),
             pltpu.VMEM((RING, 1, 128), F32),
-            dma((2, groups)),
+            dma((5,)),
             dma((2, groups)),
             dma,
             dma,
@@ -429,17 +477,18 @@
             dma((3,)),
             dma((3,)),
         ],
-        compiler_params=pltpu.CompilerParams(collective_id=0, has_side_effects=True),
+        compiler_params=pltpu.CompilerParams(collective_id=0, has_side_effects=True, vmem_limit_bytes=64880640),
         name="demo_step",
     )(
         gradient,
         momentum,
         jnp.transpose(indices.reshape(columns // BLOCK, TOPK)),
-        right_constants(cosines.T),
+        pair_constants(cosines.T),
         right_constants(cosines),
-        left_constants(cosines),
+        entry_constants(cosines),
         left_constants(cosines.T),
     )
+    return nm[None], up
 
 
 def solution(mesh):

time: 49.9 us -> 42.9 us (0.86)
  Pallas kernels: 45.7 us -> 40.2 us
  local copies, waits for them, and re-layouts: 3.32 us -> 1.94 us
    pallas_call x1, Pallas kernels: 45.7 us -> 40.2 us  [local(): pl.pallas_call(functools.partial(kernel, total_count), out_shape=(pltpu.V...]
    unnamed x4 -> x2, local copies, waits for them, and re-layouts: 3.32 us -> 1.94 us
where the time goes in v2:
time: 42.9 us; the launch traced here: 42.8 us
  Pallas kernels  40.2 us (94%)
  local copies, waits for them, and re-layouts  1.94 us (5%)
  between operations  0.64 us (1%)
    pallas_call x1, Pallas kernels, local(): pl.pallas_call(functools.partial(kernel, total_count), out_shape=(pltpu.V...  40.2 us
    unnamed x2, local copies, waits for them, and re-layouts  1.94 us

profile of v2, /device:TPU:2, one launch (start us, length us, event | category | flops | bytes accessed | tf_op | source)
XLA Modules:
  0.0 42.8 jit_solution(4319734999705924372)
XLA Ops:
  0.6 40.2 %demo_step.1 = (bf16[64,8192]{1,0:T(8,128)(2,1)S(1)}, bf16[64,8192]{1,0:T(8,128)(2,1)S(1)}) custom-call(bf16[1,64,8192]{2,1,0:T(8,128)(2,1)} %g_hbm.1, bf16[1,64,8192]{2,1,0:T(8,128)(2,1)} %m_hbm.1, s32[32,128]{1,0:T(8,128)} %bitcast.5, bf16[256,256]{1,0:T(8,128)(2,1)} %constant.8.clone.fwd_pair_hbm, bf16[2,256,256]{2,1,0:T(8,128)(2,1)} %constant.9.clone.inv_right_hbm, ...), custom_call_target="tpu_custom_call" | custom-call | tf_op jit(solution)/shard_map/demo_step/pallas_call | solution.py:443
  40.8 1.0 %copy.11 = bf16[1,64,8192]{2,1,0:T(8,128)(2,1)} copy(bf16[1,64,8192]{2,1,0:T(8,128)(2,1)S(1)} %bitcast.4) | data formatting | bytes 2097152
  41.8 1.0 %copy.12 = bf16[64,8192]{1,0:T(8,128)(2,1)} copy(bf16[64,8192]{1,0:T(8,128)(2,1)S(1)} %get-tuple-element.7) | data formatting | bytes 2097152

commit v3 on v2

v3 whole, which is shorter than its diff:
```python
import functools

import jax
import jax.numpy as jnp
import numpy as np
from jax import lax
from jax.experimental import pallas as pl
from jax.experimental.pallas import tpu as pltpu
from jax.sharding import PartitionSpec as P

MESH = pl.DeviceIdType.MESH
BLOCK = 64
TOPK = 32
CHUNK = 256
RING = 8
OWN = 4
GROUP = 8
EPSILON = 1e-06
DECAY = 0.999
F32 = jnp.float32
BF16 = jnp.bfloat16


def basis():
    frequency = np.arange(BLOCK, dtype=np.float64)[:, None]
    position = np.arange(BLOCK, dtype=np.float64)[None, :]
    waves = np.cos(np.pi * (2.0 * position + 1.0) * frequency / (2.0 * BLOCK))
    return waves * np.where(frequency == 0.0, np.sqrt(1.0 / BLOCK), np.sqrt(2.0 / BLOCK))


def halves(array):
    array = array.astype(np.float32)
    high = array.astype(BF16)
    low = (array - high.astype(np.float32)).astype(BF16)
    return high, low


def pair_constants(matrix):
    pair = np.concatenate([np.kron(np.eye(2), half.astype(np.float32)).astype(BF16) for half in halves(matrix)], axis=1)
    return np.concatenate([pair, pair], axis=0)


def entry_constants(matrix):
    return np.concatenate(
        [np.concatenate(pair, axis=1) for pair in zip(halves(DECAY * matrix), halves(matrix))], axis=0
    )


def left_constants(matrix):
    high, low = halves(matrix)
    return np.concatenate([high, high, low, low], axis=1)


def dot(a, b):
    return jnp.dot(a, b, preferred_element_type=F32)


def dot_nt(a, b):
    return lax.dot_general(a, b, (((1,), (1,)), ((), ())), preferred_element_type=F32)


def split(x):
    high = x.astype(BF16)
    return high, (x - high.astype(F32)).astype(BF16)


def left(constants, y):
    high, low = split(y)
    return dot(constants, jnp.concatenate([high, low, high, low], axis=0))


def iota(shape, dim):
    return lax.broadcasted_iota(jnp.int32, shape, dim)


def kernel(
    total_count,
    g_hbm,
    m_hbm,
    idx_hbm,
    fwd_pair_hbm,
    inv_pair_hbm,
    entry_hbm,
    inv_left_hbm,
    nm_ref,
    up_ref,
    idx_ref,
    fwd_pair,
    inv_pair,
    entry,
    inv_left,
    g_ref,
    m_ref,
    y_ref,
    s_ref,
    ob_ref,
    oa_ref,
    turned_ref,
    il_ref,
    sent_ids,
    msg_ref,
    recv_ids,
    recv_values,
    flat_ids,
    flat_values,
    part_ref,
    land_ref,
    et_ref,
    ed_ref,
    const_sem,
    in_sem,
    msg_send,
    msg_recv,
    land_send,
    land_recv,
    e_send,
    e_recv,
):
    me = lax.axis_index("dp")
    tensor = lax.axis_index("tensor")
    z, y = me // RING, lax.rem(me, RING)
    replicas = RING * RING
    chunks = ob_ref.shape[0]
    groups = chunks // GROUP
    wide = GROUP * CHUNK

    def group_columns(i):
        return pl.ds(pl.multiple_of(i * wide, wide), wide)

    def load(i, which):
        hbm, ref = ((g_hbm, g_ref), (m_hbm, m_ref))[which]
        return pltpu.make_async_copy(
            hbm.at[0, :, group_columns(i)], ref.at[:, group_columns(i)], in_sem.at[which, i]
        )

    small = [
        pltpu.make_async_copy(hbm, ref, const_sem.at[i])
        for i, (hbm, ref) in enumerate(
            [
                (idx_hbm, idx_ref),
                (entry_hbm, entry),
                (fwd_pair_hbm, fwd_pair),
                (inv_pair_hbm, inv_pair),
                (inv_left_hbm, inv_left),
            ]
        )
    ]
    for copy in small[:3]:
        copy.start()
    for i in range(groups):
        load(i, 0).start()
        load(i, 1).start()
    for copy in small[3:]:
        copy.start()

    barrier = pltpu.get_barrier_semaphore()

    def nearest(i):
        return ((i + 1) // 2) * (2 * lax.rem(i, 2) - 1)

    def far_first(i, visit, own):
        peer_z = lax.rem(z + nearest(RING - 1 - i) + RING, RING)
        for step in (4, 3, -3, 2, -2, 1, -1):
            visit(peer_z * RING + lax.rem(y + step + RING, RING))
        if not own:
            visit(peer_z * RING + y)

    def every_peer(visit):
        def row(i, carry):
            far_first(i, visit, False)
            return carry

        lax.fori_loop(0, RING - 1, row, 0)
        far_first(RING - 1, visit, True)

    def greet(peer):
        pl.semaphore_signal(barrier, inc=1, device_id={"dp": peer}, device_id_type=MESH)

    def greet_tensor(k, carry):
        pl.semaphore_signal(barrier, inc=1, device_id={"tensor": lax.rem(tensor + k, RING)}, device_id_type=MESH)
        return carry

    every_peer(greet)
    lax.fori_loop(1, RING, greet_tensor, 0)

    small[0].wait()
    turned_ref[...] = jnp.transpose(idx_ref[...])
    il_ref[...] = jnp.concatenate(
        [turned_ref[pl.ds(k, chunks, stride=4), :] for k in range(4)], axis=1
    )
    lane_span = iota((1, 128), 1) // TOPK

    def mark(chunk):
        ids = il_ref[chunk : chunk + 1, :]
        row_hit = iota((BLOCK, 128), 0) == ids // BLOCK
        col_hit = iota((CHUNK, 128), 0) == lax.rem(ids, BLOCK) + BLOCK * lane_span
        ob_ref[chunk] = jnp.where(col_hit, 1.0, 0.0).astype(BF16)
        oa_ref[chunk] = jnp.where(row_hit, 1.0, 0.0).astype(BF16)
        sent_ids[chunk // 2, chunk % 2 : chunk % 2 + 1, :] = ids

    def renewed(c):
        columns = pl.ds(pl.multiple_of(c * CHUNK, CHUNK), CHUNK)
        return DECAY * m_ref[:, columns].astype(F32) + g_ref[:, columns].astype(F32)

    small[1].wait()
    small[2].wait()

    def rows_first(i):
        load(i, 0).wait()
        load(i, 1).wait()
        for c in range(i * GROUP, (i + 1) * GROUP):
            columns = slice(c * CHUNK, (c + 1) * CHUNK)
            both = dot(entry[...], jnp.concatenate([m_ref[:, columns], g_ref[:, columns]], axis=0))
            high, low = split(both[:BLOCK] + both[BLOCK:])
            for k in range(2):
                rows = slice((2 * c + k) * BLOCK, (2 * c + k + 1) * BLOCK)
                y_ref[rows, :128] = high[:, k * 128 : (k + 1) * 128]
                y_ref[rows, 128:] = low[:, k * 128 : (k + 1) * 128]

    def columns_next(i):
        rows = slice(i * GROUP * 2 * BLOCK, (i + 1) * GROUP * 2 * BLOCK)
        both = dot(y_ref[rows, :], fwd_pair[...])
        s_ref[rows, :] = both[:, :128] + both[:, 128:]

    def spectrum_of(c):
        start = c * 2 * BLOCK
        return jnp.concatenate([s_ref[pl.ds(start, BLOCK), :], s_ref[pl.ds(start + BLOCK, BLOCK), :]], axis=1)

    def pick(i):
        for c in range(i * GROUP, (i + 1) * GROUP):
            by_column = dot(spectrum_of(c).astype(BF16), ob_ref[c])
            row = jnp.sum(by_column * oa_ref[c].astype(F32), axis=0, keepdims=True)
            if c % 2:
                msg_ref[c // 2] = jnp.concatenate([before, row], axis=0).astype(BF16)
            before = row

    for i in range(groups + 2):
        if i >= 2:
            pick(i - 2)
        if 1 <= i <= groups:
            columns_next(i - 1)
        if i < groups:
            rows_first(i)
            for c in range(i * GROUP, (i + 1) * GROUP):
                mark(c)

    pl.semaphore_wait(barrier, replicas - 1 + RING - 1)

    def owned(place):
        return lax.rem(place // RING, OWN) * OWN + lax.rem(place, OWN)

    def send_messages(peer):
        for i, (source, target) in enumerate(((sent_ids, recv_ids), (msg_ref, recv_values))):
            pltpu.make_async_remote_copy(
                src_ref=source.at[owned(peer)],
                dst_ref=target.at[me],
                send_sem=msg_send.at[i],
                recv_sem=msg_recv.at[i, z],
                device_id={"dp": peer},
                device_id_type=MESH,
            ).start()

    every_peer(send_messages)

    def paired(pieces):
        rows = []
        for piece in pieces:
            high, low = split(piece)
            for k in range(0, piece.shape[1], 128):
                rows.append(jnp.concatenate([high[:, k : k + 128], low[:, k : k + 128]], axis=1))
        both = dot(jnp.concatenate(rows, axis=0), inv_pair[...])
        both = both[:, :128] + both[:, 128:]
        return [both[k * BLOCK : (k + 1) * BLOCK] for k in range(len(rows))]

    small[3].wait()
    small[4].wait()
    mine = owned(me)
    recv_ids[me] = sent_ids[mine]
    recv_values[me] = msg_ref[mine]

    frequency = iota((BLOCK, 128), 0)
    lane_group = iota((RING, 128), 1) // TOPK
    own_group = lax.rem(iota((RING, 128), 0), 4) == lane_group

    def turns(rows):
        return [rows] + [pltpu.roll(rows, TOPK * k, 1) for k in range(1, 4)]

    def gathered(turned, k):
        out = turned[(-k) % 4]
        for g in range(1, 4):
            out = jnp.where(lane_group == g, turned[(g - k) % 4], out)
        out = jnp.where(own_group, out, jnp.zeros_like(out))
        out = out + pltpu.roll(out, 1, 0)
        return out + pltpu.roll(out, 2, 0)

    def combine(row, count):
        for i, ref in enumerate((recv_ids, recv_values)):
            arrived = ref.at[pl.ds(0, count)]
            pltpu.make_async_copy(arrived, arrived, msg_recv.at[i, row]).wait()
        flat_ids[...] = recv_ids[pl.ds(row * RING, RING)].reshape(2 * RING, 128)
        flat_values[...] = recv_values[pl.ds(row * RING, RING)].astype(F32).reshape(2 * RING, 128)
        for u in range(2):
            all_ids = turns(flat_ids[pl.ds(u, RING, stride=2), :])
            all_values = turns(flat_values[pl.ds(u, RING, stride=2), :])
            for k in range(4):
                ids, values = gathered(all_ids, k), gathered(all_values, k)
                ids_a, ids_b = ids // BLOCK, lax.rem(ids, BLOCK)
                rows, cols = [], []
                for j in (3, 7):
                    rows.append(jnp.where(frequency == ids_a[j : j + 1], values[j : j + 1], 0.0).astype(BF16))
                    cols.append(jnp.where(frequency == ids_b[j : j + 1], 1.0, 0.0).astype(BF16))
                part_ref[row, 4 * u + k] = dot_nt(jnp.concatenate(rows, axis=1), jnp.concatenate(cols, axis=1))

    combine(z, RING - 1)

    def combine_row(i, carry):
        combine(lax.rem(z + nearest(i) + RING, RING), RING)
        return carry

    lax.fori_loop(1, RING, combine_row, 0)

    def summed(k):
        total = part_ref[0, k]
        for row in range(1, RING):
            total = total + part_ref[row, k]
        return total

    combined = [jnp.concatenate([summed(k), summed(k + 1)], axis=1) for k in range(0, 8, 2)]
    energy = sum(jnp.sum(pair * pair, axis=0, keepdims=True) for pair in combined)

    def send_energy(ref, place, stage, targets):
        for target in targets:
            pltpu.make_async_remote_copy(
                src_ref=ref.at[place],
                dst_ref=ref.at[place],
                send_sem=e_send.at[stage],
                recv_sem=e_recv.at[stage],
                device_id=target,
                device_id_type=MESH,
            ).start()

    et_ref[tensor] = energy
    send_energy(et_ref, tensor, 0, [{"tensor": lax.rem(tensor + k, RING)} for k in (4, 5, 3, 2, 6, 7, 1)])

    halfway = paired(combined)
    quarter_rows = BLOCK // 4
    for k in range(2):
        decoded = left(inv_left[...], jnp.concatenate(halfway[2 * k : 2 * k + 2], axis=1))
        rounded = decoded.astype(BF16)
        for h in range(2):
            for part in range(2):
                start = (2 * h + part) * quarter_rows
                land_ref[h, mine, part, :, k * CHUNK : (k + 1) * CHUNK] = rounded[start : start + quarter_rows]

    along = ((y, z), (z, y))

    def place_of(h, a, b):
        a, b = lax.rem(a + RING, RING), lax.rem(b + RING, RING)
        return b * RING + a if h == 0 else a * RING + b

    def item_of(h, a, b):
        return owned(place_of(h, a, b))

    def send_item(h, ref, sem, target):
        pltpu.make_async_remote_copy(
            src_ref=ref,
            dst_ref=ref,
            send_sem=land_send.at[h],
            recv_sem=sem,
            device_id={"dp": target},
            device_id_type=MESH,
        ).start()

    def spread(h, item, places):
        for step, place in zip((1, -1), places[:2]):
            send_item(h, land_ref.at[h, item], land_recv.at[h, item, 0], place)
        for part, place in enumerate(places[2:]):
            send_item(h, land_ref.at[h, item, part], land_recv.at[h, item, part], place)

    def spread_first(h):
        a, b = along[h]
        spread(h, mine, [place_of(h, a + step, b) for step in (1, -1, 2, -2)])

    def spread_second(h, item):
        a, b = along[h]
        spread(h, item, [place_of(h, a, b + step) for step in (1, -1, 2, -2)])

    def wait_whole(h, item):
        ref = land_ref.at[h, item]
        pltpu.make_async_copy(ref, ref, land_recv.at[h, item, 0]).wait()

    def wait_parts(h, item):
        for part in range(2):
            ref = land_ref.at[h, item, part]
            pltpu.make_async_copy(ref, ref, land_recv.at[h, item, part]).wait()

    def take_energy(ref, stage, count):
        rest = ref.at[pl.ds(0, count - 1)]
        pltpu.make_async_copy(rest, rest, e_recv.at[stage]).wait()
        pltpu.make_async_copy(rest, rest, e_send.at[stage]).wait()
        row = ref[0]
        for k in range(1, count):
            row = row + ref[k]
        return row

    for h in range(2):
        spread_first(h)
    for h in range(2):
        spread_second(h, mine)
    for step in (1, -1):
        for h in range(2):
            a, b = along[h]
            item = item_of(h, a + step, b)
            wait_whole(h, item)
            spread_second(h, item)
    ed_ref[mine] = take_energy(et_ref, 0, RING)
    near = [(i, j) for i in (-1, 0, 1, 2) for j in (-1, 0, 1, 2) if (i, j) != (0, 0)]
    send_energy(ed_ref, mine, 1, [{"dp": place_of(0, y + i, z + j)} for i, j in near])
    for h in range(2):
        a, b = along[h]
        item = item_of(h, a + 2, b)
        wait_parts(h, item)
        spread_second(h, item)

    def remove(i, carry):
        rows = []
        for c in range(GROUP):
            chunk = i * GROUP + c
            marker = dot_nt(oa_ref[chunk], ob_ref[chunk])
            rows.append(left(inv_left[...], spectrum_of(chunk) * marker))
        restored = paired(rows)
        for c in range(GROUP):
            chunk = i * GROUP + c
            columns = pl.ds(pl.multiple_of(chunk * CHUNK, CHUNK), CHUNK)
            taken = jnp.concatenate(restored[2 * c : 2 * c + 2], axis=1)
            nm_ref[:, columns] = (renewed(chunk) - taken).astype(BF16)
        return carry

    lax.fori_loop(0, groups, remove, 0)

    energy = jnp.sum(take_energy(ed_ref, 1, OWN * OWN), axis=1, keepdims=True)
    scale = 1.0 / jnp.sqrt(energy / total_count + EPSILON)

    def finish(h, item):
        columns = pl.ds(pl.multiple_of(item * 2 * CHUNK, 2 * CHUNK), 2 * CHUNK)
        for part in range(2):
            start = (2 * h + part) * quarter_rows
            up_ref[start : start + quarter_rows, columns] = (
                land_ref[h, item, part].astype(F32) * scale
            ).astype(BF16)

    steps = (0, 1, -1, 2)
    for other in steps:
        for step in steps:
            for h in range(2):
                a, b = along[h]
                item = item_of(h, a + step, b + other)
                if other in (1, -1):
                    wait_whole(h, item)
                elif other == 2:
                    wait_parts(h, item)
                finish(h, item)

    for i, ref in enumerate((recv_ids, recv_values)):
        others = ref.at[pl.ds(0, replicas - 1)]
        pltpu.make_async_copy(others, others, msg_send.at[i]).wait()
    for h in range(2):
        rest = land_ref.at[h, pl.ds(0, OWN * OWN - 1)]
        pltpu.make_async_copy(rest, rest, land_send.at[h]).wait()


def deliver(nm_ref, up_ref, nm_hbm, up_hbm, sem):
    copies = [
        pltpu.make_async_copy(nm_ref, nm_hbm.at[0], sem.at[0]),
        pltpu.make_async_copy(up_ref, up_hbm, sem.at[1]),
    ]
    for copy in copies:
        copy.start()
    for copy in copies:
        copy.wait()


def local(total_count, gradient, momentum, indices):
    _, height, columns = gradient.shape
    chunks = columns // CHUNK
    groups = chunks // GROUP
    replicas = RING * RING
    cosines = basis()
    anywhere = pl.BlockSpec(memory_space=pl.ANY)
    dma = pltpu.SemaphoreType.DMA
    nm, up = pl.pallas_call(
        functools.partial(kernel, total_count),
        out_shape=(
            pltpu.VMEM((height, columns), BF16),
            pltpu.VMEM((height, columns), BF16),
        ),
        in_specs=[anywhere] * 7,
        out_specs=(pl.BlockSpec(memory_space=pltpu.VMEM),) * 2,
        scratch_shapes=[
            pltpu.VMEM((TOPK, columns // BLOCK), jnp.int32),
            pltpu.VMEM((256, 256), BF16),
            pltpu.VMEM((256, 256), BF16),
            pltpu.VMEM((128, 128), BF16),
            pltpu.VMEM((BLOCK, 256), BF16),
            pltpu.VMEM((height, columns), BF16),
            pltpu.VMEM((height, columns), BF16),
            pltpu.VMEM((chunks * 2 * BLOCK, 256), BF16),
            pltpu.VMEM((chunks * 2 * BLOCK, 128), F32),
            pltpu.VMEM((chunks, CHUNK, 128), BF16),
            pltpu.VMEM((chunks, BLOCK, 128), BF16),
            pltpu.VMEM((chunks * 4, TOPK), jnp.int32),
            pltpu.VMEM((chunks, 128), jnp.int32),
            pltpu.VMEM((OWN * OWN, 2, 128), jnp.int32),
            pltpu.VMEM((OWN * OWN, 2, 128), BF16),
            pltpu.VMEM((replicas, 2, 128), jnp.int32),
            pltpu.VMEM((replicas, 2, 128), BF16),
            pltpu.VMEM((2 * RING, 128), jnp.int32),
            pltpu.VMEM((2 * RING, 128), F32),
            pltpu.VMEM((RING, 8, BLOCK, BLOCK), F32),
            pltpu.VMEM((2, OWN * OWN, 2, BLOCK // 4, 2 * CHUNK), BF16),
            pltpu.VMEM((RING, 1, 128), F32),
            pltpu.VMEM((OWN * OWN, 1, 128), F32),
            dma((5,)),
            dma((2, groups)),
            dma((2,)),
            dma((2, RING)),
            dma((2,)),
            dma((2, OWN * OWN, 2)),
            dma((2,)),
            dma((2,)),
        ],
        compiler_params=pltpu.CompilerParams(collective_id=0, has_side_effects=True, vmem_limit_bytes=64880640),
        name="demo_step",
    )(
        gradient,
        momentum,
        jnp.transpose(indices.reshape(columns // BLOCK, TOPK)),
        pair_constants(cosines.T),
        pair_constants(cosines),
        entry_constants(cosines),
        left_constants(cosines.T),
    )
    return pl.pallas_call(
        deliver,
        out_shape=(
            jax.ShapeDtypeStruct((1, height, columns), BF16),
            jax.ShapeDtypeStruct((height, columns), BF16),
        ),
        in_specs=[pl.BlockSpec(memory_space=pltpu.VMEM)] * 2,
        out_specs=(anywhere, anywhere),
        scratch_shapes=[dma((2,))],
        compiler_params=pltpu.CompilerParams(vmem_limit_bytes=2**20),
        name="deliver",
    )(nm, up)


def solution(mesh):
    def whole(gradient, momentum, indices):
        rows, columns = gradient.shape[1:]
        return jax.shard_map(
            functools.partial(local, float(rows * columns)),
            mesh=mesh,
            in_specs=(P("dp", "tensor", None), P("dp", "tensor", None), P("dp", "tensor", None, None)),
            out_specs=(P("dp", "tensor", None), P("tensor", None)),
            check_vma=False,
        )(gradient, momentum, indices)

    return whole
```

time: 42.9 us -> 37.8 us (0.88)
  the two profiles are of different devices: /device:TPU:2 before, /device:TPU:8 now
where the time goes in v3:
time: 37.8 us; the launch traced here: 37.7 us
  Pallas kernels  37 us (98%)
  between operations  0.64 us (2%)
    pallas_call x1, Pallas kernels, local(): pl.pallas_call(functools.partial(kernel, total_count), out_shape=(pltpu.V...  35.7 us
    pallas_call x1, Pallas kernels, local(): pl.pallas_call(deliver, out_shape=(jax.ShapeDtypeStruct((1, height, colum...  1.33 us

profile of v3, /device:TPU:8, one launch (start us, length us, event | category | flops | bytes accessed | tf_op | source)
XLA Modules:
  0.0 37.7 jit_solution(15597077546169523168)
XLA Ops:
  0.6 35.7 %demo_step.1 = (bf16[64,8192]{1,0:T(8,128)(2,1)S(1)}, bf16[64,8192]{1,0:T(8,128)(2,1)S(1)}) custom-call(bf16[1,64,8192]{2,1,0:T(8,128)(2,1)} %g_hbm.1, bf16[1,64,8192]{2,1,0:T(8,128)(2,1)} %m_hbm.1, s32[32,128]{1,0:T(8,128)} %bitcast.3, bf16[256,256]{1,0:T(8,128)(2,1)} %constant.8.clone.fwd_pair_hbm, bf16[256,256]{1,0:T(8,128)(2,1)} %constant.9.clone.inv_pair_hbm, ...), custom_call_target="tpu_custom_call" | custom-call | tf_op jit(solution)/shard_map/demo_step/pallas_call | solution.py:491
  36.3 1.3 %deliver.1 = (bf16[1,64,8192]{2,1,0:T(8,128)(2,1)}, bf16[64,8192]{1,0:T(8,128)(2,1)}) custom-call(bf16[64,8192]{1,0:T(8,128)(2,1)S(1)} %get-tuple-element.4.nm_ref, bf16[64,8192]{1,0:T(8,128)(2,1)S(1)} %get-tuple-element.5.up_ref), custom_call_target="tpu_custom_call" | custom-call | tf_op jit(solution)/shard_map/deliver/pallas_call | solution.py:543

commit v4 on v3

--- a/solution.py
+++ b/solution.py
@@ -14,7 +14,7 @@
 CHUNK = 256
 RING = 8
 OWN = 4
-GROUP = 8
+GROUP = 16
 EPSILON = 1e-06
 DECAY = 0.999
 F32 = jnp.float32
@@ -371,28 +371,23 @@
             device_id_type=MESH,
         ).start()
 
-    def spread(h, item, places):
-        for step, place in zip((1, -1), places[:2]):
-            send_item(h, land_ref.at[h, item], land_recv.at[h, item, 0], place)
+    def spread(h, turn, item, places):
+        for side, place in enumerate(places[:2]):
+            send_item(h, land_ref.at[h, item], land_recv.at[h, turn, side], place)
         for part, place in enumerate(places[2:]):
-            send_item(h, land_ref.at[h, item, part], land_recv.at[h, item, part], place)
+            send_item(h, land_ref.at[h, item, part], land_recv.at[h, turn, 2], place)
 
     def spread_first(h):
         a, b = along[h]
-        spread(h, mine, [place_of(h, a + step, b) for step in (1, -1, 2, -2)])
+        spread(h, 0, mine, [place_of(h, a + step, b) for step in (1, -1, 2, -2)])
 
     def spread_second(h, item):
         a, b = along[h]
-        spread(h, item, [place_of(h, a, b + step) for step in (1, -1, 2, -2)])
-
-    def wait_whole(h, item):
-        ref = land_ref.at[h, item]
-        pltpu.make_async_copy(ref, ref, land_recv.at[h, item, 0]).wait()
-
-    def wait_parts(h, item):
-        for part in range(2):
-            ref = land_ref.at[h, item, part]
-            pltpu.make_async_copy(ref, ref, land_recv.at[h, item, part]).wait()
+        spread(h, 1, item, [place_of(h, a, b + step) for step in (1, -1, 2, -2)])
+
+    def wait_items(h, turn, side, count):
+        ref = land_ref.at[h, pl.ds(0, count)]
+        pltpu.make_async_copy(ref, ref, land_recv.at[h, turn, side]).wait()
 
     def take_energy(ref, stage, count):
         rest = ref.at[pl.ds(0, count - 1)]
@@ -407,20 +402,18 @@
         spread_first(h)
     for h in range(2):
         spread_second(h, mine)
-    for step in (1, -1):
+    for side, step in enumerate((-1, 1)):
         for h in range(2):
             a, b = along[h]
-            item = item_of(h, a + step, b)
-            wait_whole(h, item)
-            spread_second(h, item)
+            wait_items(h, 0, side, 1)
+            spread_second(h, item_of(h, a + step, b))
     ed_ref[mine] = take_energy(et_ref, 0, RING)
     near = [(i, j) for i in (-1, 0, 1, 2) for j in (-1, 0, 1, 2) if (i, j) != (0, 0)]
     send_energy(ed_ref, mine, 1, [{"dp": place_of(0, y + i, z + j)} for i, j in near])
     for h in range(2):
         a, b = along[h]
-        item = item_of(h, a + 2, b)
-        wait_parts(h, item)
-        spread_second(h, item)
+        wait_items(h, 0, 2, 1)
+        spread_second(h, item_of(h, a + 2, b))
 
     def remove(i, carry):
         rows = []
@@ -449,17 +442,13 @@
                 land_ref[h, item, part].astype(F32) * scale
             ).astype(BF16)
 
-    steps = (0, 1, -1, 2)
-    for other in steps:
-        for step in steps:
-            for h in range(2):
-                a, b = along[h]
-                item = item_of(h, a + step, b + other)
-                if other in (1, -1):
-                    wait_whole(h, item)
-                elif other == 2:
-                    wait_parts(h, item)
-                finish(h, item)
+    for side, other in ((None, 0), (0, -1), (1, 1), (2, 2)):
+        for h in range(2):
+            a, b = along[h]
+            if side is not None:
+                wait_items(h, 1, side, OWN)
+            for step in (0, 1, -1, 2):
+                finish(h, item_of(h, a + step, b + other))
 
     for i, ref in enumerate((recv_ids, recv_values)):
         others = ref.at[pl.ds(0, replicas - 1)]
@@ -525,7 +514,7 @@
             dma((2,)),
             dma((2, RING)),
             dma((2,)),
-            dma((2, OWN * OWN, 2)),
+            dma((2, 2, 3)),
             dma((2,)),
             dma((2,)),
         ],

time: 37.8 us -> 36.5 us (0.966)
  the two profiles are of different devices: /device:TPU:8 before, /device:TPU:2 now
where the time goes in v4:
time: 36.5 us; the launch traced here: 36.3 us
  Pallas kernels  35.6 us (98%)
  between operations  0.64 us (2%)
    pallas_call x1, Pallas kernels, local(): pl.pallas_call(functools.partial(kernel, total_count), out_shape=(pltpu.V...  34.3 us
    pallas_call x1, Pallas kernels, local(): pl.pallas_call(deliver, out_shape=(jax.ShapeDtypeStruct((1, height, colum...  1.33 us

profile of v4, /device:TPU:2, one launch (start us, length us, event | category | flops | bytes accessed | tf_op | source)
XLA Modules:
  0.0 36.3 jit_solution(10153399615977859008)
XLA Ops:
  0.6 34.3 %demo_step.1 = (bf16[64,8192]{1,0:T(8,128)(2,1)S(1)}, bf16[64,8192]{1,0:T(8,128)(2,1)S(1)}) custom-call(bf16[1,64,8192]{2,1,0:T(8,128)(2,1)} %g_hbm.1, bf16[1,64,8192]{2,1,0:T(8,128)(2,1)} %m_hbm.1, s32[32,128]{1,0:T(8,128)} %bitcast.3, bf16[256,256]{1,0:T(8,128)(2,1)} %constant.8.clone.fwd_pair_hbm, bf16[256,256]{1,0:T(8,128)(2,1)} %constant.9.clone.inv_pair_hbm, ...), custom_call_target="tpu_custom_call" | custom-call | tf_op jit(solution)/shard_map/demo_step/pallas_call | solution.py:480
  34.9 1.3 %deliver.1 = (bf16[1,64,8192]{2,1,0:T(8,128)(2,1)}, bf16[64,8192]{1,0:T(8,128)(2,1)}) custom-call(bf16[64,8192]{1,0:T(8,128)(2,1)S(1)} %get-tuple-element.4.nm_ref, bf16[64,8192]{1,0:T(8,128)(2,1)S(1)} %get-tuple-element.5.up_ref), custom_call_target="tpu_custom_call" | custom-call | tf_op jit(solution)/shard_map/deliver/pallas_call | solution.py:532

commit v5 on v4

--- a/solution.py
+++ b/solution.py
@@ -14,7 +14,7 @@
 CHUNK = 256
 RING = 8
 OWN = 4
-GROUP = 16
+GROUP = 32
 EPSILON = 1e-06
 DECAY = 0.999
 F32 = jnp.float32
@@ -293,15 +293,17 @@
         out = out + pltpu.roll(out, 1, 0)
         return out + pltpu.roll(out, 2, 0)
 
-    def combine(row, count):
+    def arrive(row, count):
         for i, ref in enumerate((recv_ids, recv_values)):
             arrived = ref.at[pl.ds(0, count)]
             pltpu.make_async_copy(arrived, arrived, msg_recv.at[i, row]).wait()
-        flat_ids[...] = recv_ids[pl.ds(row * RING, RING)].reshape(2 * RING, 128)
-        flat_values[...] = recv_values[pl.ds(row * RING, RING)].astype(F32).reshape(2 * RING, 128)
+
+    def combine(row, slot):
+        flat_ids[slot] = recv_ids[pl.ds(row * RING, RING)].reshape(2 * RING, 128)
+        flat_values[slot] = recv_values[pl.ds(row * RING, RING)].astype(F32).reshape(2 * RING, 128)
         for u in range(2):
-            all_ids = turns(flat_ids[pl.ds(u, RING, stride=2), :])
-            all_values = turns(flat_values[pl.ds(u, RING, stride=2), :])
+            all_ids = turns(flat_ids[slot, pl.ds(u, RING, stride=2), :])
+            all_values = turns(flat_values[slot, pl.ds(u, RING, stride=2), :])
             for k in range(4):
                 ids, values = gathered(all_ids, k), gathered(all_values, k)
                 ids_a, ids_b = ids // BLOCK, lax.rem(ids, BLOCK)
@@ -311,13 +313,20 @@
                     cols.append(jnp.where(frequency == ids_b[j : j + 1], 1.0, 0.0).astype(BF16))
                 part_ref[row, 4 * u + k] = dot_nt(jnp.concatenate(rows, axis=1), jnp.concatenate(cols, axis=1))
 
-    combine(z, RING - 1)
-
-    def combine_row(i, carry):
-        combine(lax.rem(z + nearest(i) + RING, RING), RING)
+    arrive(z, RING - 1)
+    combine(z, 0)
+
+    def combine_pair(k, carry):
+        pair = (lax.rem(z + k, RING), lax.rem(z + RING - k, RING))
+        for row in pair:
+            arrive(row, RING)
+        for slot, row in enumerate(pair):
+            combine(row, slot)
         return carry
 
-    lax.fori_loop(1, RING, combine_row, 0)
+    lax.fori_loop(1, RING // 2, combine_pair, 0)
+    arrive(lax.rem(z + RING // 2, RING), RING)
+    combine(lax.rem(z + RING // 2, RING), 0)
 
     def summed(k):
         total = part_ref[0, k]
@@ -407,29 +416,29 @@
             a, b = along[h]
             wait_items(h, 0, side, 1)
             spread_second(h, item_of(h, a + step, b))
-    ed_ref[mine] = take_energy(et_ref, 0, RING)
-    near = [(i, j) for i in (-1, 0, 1, 2) for j in (-1, 0, 1, 2) if (i, j) != (0, 0)]
-    send_energy(ed_ref, mine, 1, [{"dp": place_of(0, y + i, z + j)} for i, j in near])
     for h in range(2):
         a, b = along[h]
         wait_items(h, 0, 2, 1)
         spread_second(h, item_of(h, a + 2, b))
+    ed_ref[mine] = take_energy(et_ref, 0, RING)
+    near = [(i, j) for i in (-1, 0, 1, 2) for j in (-1, 0, 1, 2) if (i, j) != (0, 0)]
+    send_energy(ed_ref, mine, 1, [{"dp": place_of(0, y + i, z + j)} for i, j in near])
 
     def remove(i, carry):
         rows = []
-        for c in range(GROUP):
-            chunk = i * GROUP + c
+        for c in range(GROUP // 2):
+            chunk = i * (GROUP // 2) + c
             marker = dot_nt(oa_ref[chunk], ob_ref[chunk])
             rows.append(left(inv_left[...], spectrum_of(chunk) * marker))
         restored = paired(rows)
-        for c in range(GROUP):
-            chunk = i * GROUP + c
+        for c in range(GROUP // 2):
+            chunk = i * (GROUP // 2) + c
             columns = pl.ds(pl.multiple_of(chunk * CHUNK, CHUNK), CHUNK)
             taken = jnp.concatenate(restored[2 * c : 2 * c + 2], axis=1)
             nm_ref[:, columns] = (renewed(chunk) - taken).astype(BF16)
         return carry
 
-    lax.fori_loop(0, groups, remove, 0)
+    lax.fori_loop(0, 2 * groups, remove, 0)
 
     energy = jnp.sum(take_energy(ed_ref, 1, OWN * OWN), axis=1, keepdims=True)
     scale = 1.0 / jnp.sqrt(energy / total_count + EPSILON)
@@ -503,8 +512,8 @@
             pltpu.VMEM((OWN * OWN, 2, 128), BF16),
             pltpu.VMEM((replicas, 2, 128), jnp.int32),
             pltpu.VMEM((replicas, 2, 128), BF16),
-            pltpu.VMEM((2 * RING, 128), jnp.int32),
-            pltpu.VMEM((2 * RING, 128), F32),
+            pltpu.VMEM((2, 2 * RING, 128), jnp.int32),
+            pltpu.VMEM((2, 2 * RING, 128), F32),
             pltpu.VMEM((RING, 8, BLOCK, BLOCK), F32),
             pltpu.VMEM((2, OWN * OWN, 2, BLOCK // 4, 2 * CHUNK), BF16),
             pltpu.VMEM((RING, 1, 128), F32),

time: 36.5 us -> 37.1 us (1.016)
  Pallas kernels: 35.6 us -> 36.3 us
    pallas_call x1, Pallas kernels: 34.3 us -> 34.9 us  [local(): pl.pallas_call(functools.partial(kernel, total_count), out_shape=(pltpu.V...]
where the time goes in v5:
time: 37.1 us; the launch traced here: 36.9 us
  Pallas kernels  36.3 us (98%)
  between operations  0.64 us (2%)
    pallas_call x1, Pallas kernels, local(): pl.pallas_call(functools.partial(kernel, total_count), out_shape=(pltpu.V...  34.9 us
    pallas_call x1, Pallas kernels, local(): pl.pallas_call(deliver, out_shape=(jax.ShapeDtypeStruct((1, height, colum...  1.33 us

profile of v5, /device:TPU:2, one launch (start us, length us, event | category | flops | bytes accessed | tf_op | source)
XLA Modules:
  0.0 36.9 jit_solution(3585274660249176159)
XLA Ops:
  0.6 34.9 %demo_step.1 = (bf16[64,8192]{1,0:T(8,128)(2,1)S(1)}, bf16[64,8192]{1,0:T(8,128)(2,1)S(1)}) custom-call(bf16[1,64,8192]{2,1,0:T(8,128)(2,1)} %g_hbm.1, bf16[1,64,8192]{2,1,0:T(8,128)(2,1)} %m_hbm.1, s32[32,128]{1,0:T(8,128)} %bitcast.3, bf16[256,256]{1,0:T(8,128)(2,1)} %constant.8.clone.fwd_pair_hbm, bf16[256,256]{1,0:T(8,128)(2,1)} %constant.9.clone.inv_pair_hbm, ...), custom_call_target="tpu_custom_call" | custom-call | tf_op jit(solution)/shard_map/demo_step/pallas_call | solution.py:489
  35.6 1.3 %deliver.1 = (bf16[1,64,8192]{2,1,0:T(8,128)(2,1)}, bf16[64,8192]{1,0:T(8,128)(2,1)}) custom-call(bf16[64,8192]{1,0:T(8,128)(2,1)S(1)} %get-tuple-element.4.nm_ref, bf16[64,8192]{1,0:T(8,128)(2,1)S(1)} %get-tuple-element.5.up_ref), custom_call_target="tpu_custom_call" | custom-call | tf_op jit(solution)/shard_map/deliver/pallas_call | solution.py:541
